TPU v7x, 32 devices: a whole 2x2x4 slice. The times are simulated.
32 devices in a mesh: dp: 4 (over x, y), tp: 8 (over z, core).
Axes of the slice: x: 2, y: 2, z: 4, core: 2. Of those that a mesh axis runs over, the one named last changes fastest.
Arguments:
- x: bfloat16 [11264, 3072], P(('dp', 'tp')), parts along dimension 0
- w_gate: bfloat16 [3072, 24576], P(None, 'tp')
- w_up: bfloat16 [3072, 24576], P(None, 'tp')
- w_down: bfloat16 [24576, 3072], P('tp')
Outputs:
- output: bfloat16 [11264, 3072], P(('dp', 'tp')), parts along dimension 0
There are 4 independent parts. A program takes and returns all parts, laid end to end along the dimension named above; an argument that names none is the same for every part.
All inputs are finite; a program needn't handle non-finite values.
Results may differ from a plain program's by a relative error of at most 0.016.
Values are sent between devices in bfloat16 or wider.
A program may use at most 2 GiB of HBM per device.

v0:
```python
import jax
import jax.numpy as jnp
from jax import lax
from jax.sharding import PartitionSpec as P


def solution(mesh):
    def step(x, w_gate, w_up, w_down):
        rows = lax.all_gather(x, "tp", axis=0, tiled=True)
        gate = jnp.dot(rows, w_gate, preferred_element_type=jnp.float32)
        up = jnp.dot(rows, w_up, preferred_element_type=jnp.float32)
        hidden = (jax.nn.gelu(gate) * up).astype(jnp.bfloat16)
        term = jnp.dot(hidden, w_down, preferred_element_type=jnp.float32).astype(jnp.bfloat16)
        return lax.psum_scatter(term, "tp", scatter_dimension=0, tiled=True)

    return jax.shard_map(
        step,
        mesh=mesh,
        in_specs=(P(("dp", "tp"), None), P(None, "tp"), P(None, "tp"), P("tp", None)),
        out_specs=P(("dp", "tp"), None),
        check_vma=False,
    )
```

profile of v0, /device:TPU:0, one launch (start us, length us, event | category | flops | bytes accessed | tf_op | source)
XLA Modules:
  0.0 545.0 jit_solution(3090283243434010024)
XLA Ops:
  6.5 0.0 all-gather.2.cloned.1.call-start
  6.5 0.7 all-gather.2.cloned.1.call-update
  7.3 0.0 reduce-scatter.2.cloned.1.call-start
  7.3 159.8 %all-gather.2.cloned.1.call-done = bf16[2816,3072]{1,0:T(8,128)(2,1)} async-done(((bf16[352,3072]{1,0:T(8,128)(2,1)}), bf16[2816,3072]{1,0:T(8,128)(2,1)}) %all-gather.2.cloned.1.call-update) | async-done | bytes 17301520 | tf_op jit(solution)/shard_map/all_gather | solution.py:9
  167.1 62.6 %fusion.9 = f32[2816,3072]{1,0:T(8,128)} fusion(bf16[2816,3072]{1,0:T(8,128)(2,1)} %all-gather.2.cloned.1.call-done, bf16[3072,3072]{1,0:T(8,128)(2,1)} %param.5), kind=kOutput, calls=%fused_computation.11 | convolution fusion | flops 53150220288 | bytes 70778880 | tf_op jit(solution)/shard_map/dot_general | solution.py:10
  229.7 74.0 %fusion.8 = bf16[2816,3072]{1,0:T(8,128)(2,1)} fusion(f32[2816,3072]{1,0:T(8,128)} %fusion.9, bf16[2816,3072]{1,0:T(8,128)(2,1)} %all-gather.2.cloned.1.call-done, bf16[3072,3072]{1,0:T(8,128)(2,1)} %param.6), kind=kOutput, calls=%fused_computation.9 | convolution fusion | flops 53236727808 | bytes 88080384 | tf_op jit(solution)/shard_map/dot_general | solution.py:11
  303.6 62.7 %convolution_convert_fusion = bf16[2816,3072]{1,0:T(8,128)(2,1)} fusion(bf16[2816,3072]{1,0:T(8,128)(2,1)} %fusion.8, bf16[3072,3072]{1,0:T(8,128)(2,1)} %param.7), kind=kOutput, calls=%fused_computation.10 | convolution fusion | flops 53158871040 | bytes 53477376 | tf_op jit(solution)/shard_map/dot_general | solution.py:13
  366.4 0.0 reduce-scatter.2.cloned.1.call-update
  366.4 171.8 %reduce-scatter.2.cloned.1.call-done = bf16[352,3072]{1,0:T(8,128)(2,1)} async-done(((bf16[2816,3072]{1,0:T(8,128)(2,1)}), bf16[352,3072]{1,0:T(8,128)(2,1)}) %reduce-scatter.2.cloned.1.call-update) | async-done | bytes 2162704 | tf_op jit(solution)/shard_map/reduce_scatter | solution.py:14
Async XLA Ops:
  6.5 160.5 %all-gather.2.cloned.1.call-start = ((), (), s32[]{:S(2)}) async-start(), calls=%async_computation.1 | async-start | bytes 19464192 | tf_op jit(solution)/shard_map/all_gather | solution.py:9
  7.3 530.9 %reduce-scatter.2.cloned.1.call-start = ((), (), s32[]{:S(2)}) async-start(), calls=%async_computation.2 | async-start | bytes 19464192 | tf_op jit(solution)/shard_map/reduce_scatter | solution.py:14
Sparse Core Ops, SparseCore 0:
  9.0 158.0 all-gather.1
  366.5 171.6 reduce-scatter.1
where the time goes:
time: 545 us
  waiting for transfers between devices  332 us (61%)
  matrix products  199 us (37%)
  between operations  13.4 us (2%)
    reduce_scatter x1, waiting for transfers between devices, step(): return lax.psum_scatter(term, 'tp', scatter_dimension=0, tiled=True)  172 us
    all_gather x1, waiting for transfers between devices, step(): rows = lax.all_gather(x, 'tp', axis=0, tiled=True)  160 us
    dot_general x1, matrix products, step(): up = jnp.dot(rows, w_up, preferred_element_type=jnp.float32)  74 us
    dot_general x1, matrix products, step(): jnp.dot(hidden, w_down, preferred_element_type=jnp.float32)  62.7 us
    dot_general x1, matrix products, step(): gate = jnp.dot(rows, w_gate, preferred_element_type=jnp.float32)  62.6 us
  transfers between devices with their start and end apart: 2, of which 2 were waited for; matrix products, arithmetic and copies ran while one was open for 0% of the time, Pallas kernels for 0%

commit v1 on v0

v1 whole, which is shorter than its diff:
```python
import functools

import jax
import jax.numpy as jnp
from jax import lax
from jax.experimental import pallas as pl
from jax.experimental.pallas import tpu as pltpu
from jax.sharding import PartitionSpec as P

CHIPS = 4
SLOTS = 2 * CHIPS
TILES = 6
HALF = TILES // 2
DELAY = 1
LAST = 2 * (SLOTS - 1) + 1 + DELAY


def mirror(item):
    return 6 - item + 2 * lax.rem(item, 2)


def gather_item(line, unit):
    slot = lax.div(unit, 2)
    item = jnp.where(slot <= line, 2 * (line - slot), 2 * (slot - line) - 1)
    return (line <= CHIPS - 2) & (slot < 2 * line + 2), item, lax.rem(unit, 2)


def sum_item(line, unit):
    slot = lax.div(unit - DELAY, 2)
    at, ahead = slot - (2 * line + 2), CHIPS - 1 - line
    item = jnp.where(at < ahead, 2 * (line + 1 + at), 2 * (CHIPS - 1 - (at - ahead)) + 1)
    valid = (line <= CHIPS - 2) & (at >= 0) & (slot < SLOTS)
    return valid, item, lax.rem(unit - DELAY, 2)


def kernel(
    x, wg, wu, wd, y, xg, stash, part, from_left, from_right,
    xv, hv, wgv, wuv, wdv, pst, sst, c_own, c_part, c_up, c_out,
    x_sem, w_sem, wd_sem, first_sem, ag_recv, d2d_recv, d2d_send, send, part_send, part_recv,
    stash_sem, load_sem, sum_recv, y_local, y_send, y_recv,
):
    rows, depth = x.shape
    ft, nt = wg.shape[1] // TILES, wd.shape[1] // TILES
    quarter, half_rows = rows // 4, rows // 2
    me = lax.axis_index("tp")
    z, c = lax.div(me, 2), lax.rem(me, 2)
    partner = me + 1 - 2 * c
    own, other = me, partner
    lines = (z, CHIPS - 1 - z)
    sources = (z - 1, CHIPS - 2 - z)
    targets = (me + 2, me - 2)
    sums = (from_left, from_right)

    def oriented(d, item):
        return item if d == 0 else mirror(item)

    def remote(src, dst, ssem, rsem, device):
        return pltpu.make_async_remote_copy(
            src_ref=src, dst_ref=dst, send_sem=ssem, recv_sem=rsem,
            device_id={"tp": device}, device_id_type=pl.DeviceIdType.MESH,
        )

    def rows_of(half, core):
        return pl.ds(pl.multiple_of((2 * half + core) * quarter, 8), quarter)

    def chunk(half):
        return pl.ds(pl.multiple_of(half * half_rows, 16), half_rows)

    def columns(i, size):
        return pl.ds(pl.multiple_of(i * size, size), size)

    def gather_copy(d, item, half, unit, src):
        return remote(src, xg.at[item, rows_of(half, c)], send.at[d, lax.rem(unit, 2)], ag_recv.at[item, half], targets[d])

    def start_gather(d, item, half, unit):
        @pl.when(item == own)
        def _():
            gather_copy(d, item, half, unit, x.at[rows_of(half, c)]).start()

        @pl.when(item != own)
        def _():
            gather_copy(d, item, half, unit, xg.at[item, rows_of(half, c)]).start()

    def wait_gathered(item, half):
        gather_copy(0, item, half, 0, xg.at[item, rows_of(half, c)]).wait_recv()

    def pass_on(d, item, half, unit, core):
        at = xg.at[item, rows_of(half, core)]
        return remote(at, at, d2d_send.at[d, lax.rem(unit, 2)], d2d_recv.at[item, half], partner)

    def sends(d, unit):
        a, _, _ = gather_item(lines[d], unit)
        b, _, _ = sum_item(lines[d], unit)
        return a | b

    def gather_service(v):
        for d in range(2):
            valid, item, half = gather_item(sources[d], v - 2)
            item = oriented(d, item)

            @pl.when(valid & (v >= 2))
            def _():
                pass_on(d, item, half, v - 2, c).wait_send()

            valid, item, half = gather_item(sources[d], v - 1)
            item = oriented(d, item)

            @pl.when(valid)
            def _():
                wait_gathered(item, half)
                pass_on(d, item, half, v - 1, c).start()

        for d in range(2):

            @pl.when(sends(d, v - 1))
            def _():
                gather_copy(d, own, 0, v - 1, xg.at[own, rows_of(0, c)]).wait_send()

            valid, item, half = gather_item(lines[d], v + 1)
            item = oriented(d, item)

            @pl.when(valid)
            def _():
                start_gather(d, item, half, v + 1)

    def loads(d, item, half, slot, n_up, ups):
        pairs = [(stash.at[item, :, chunk(half)], c_own.at[slot]), (part.at[item, :, chunk(half)], c_part.at[slot])]
        pairs += [(sums[up].at[item, :, chunk(half)], c_up.at[slot, up]) for up in ups]
        return [pltpu.make_async_copy(a, b, load_sem.at[slot, i]) for i, (a, b) in enumerate(pairs)]

    def part_copy(item, device, t, sem):
        return remote(pst.at[t], part.at[item, t], sem, part_recv.at[item], device)

    def wait_part(item):
        remote(part.at[item], part.at[item], part_send.at[0], part_recv.at[item], partner).wait_recv()

    def sum_copy(d, item, half, unit):
        return remote(
            c_out.at[d, lax.rem(unit, 2)], sums[d].at[item, :, chunk(half)],
            send.at[d, lax.rem(unit, 2)], sum_recv.at[d, item, half], targets[d],
        )

    def add(slot, out_slot, ups):
        @pl.loop(0, half_rows // 16)
        def _(i):
            at = pl.ds(pl.multiple_of(i * 16, 16), 16)
            total = c_own[slot, :, at, :] + c_part[slot, :, at, :].astype(jnp.float32)
            for up in ups:
                total += c_up[slot, up, :, at, :].astype(jnp.float32)
            c_out[slot, out_slot, :, at, :] = total.astype(jnp.bfloat16)

    def sum_cases(d, v, act):
        valid, item, half = sum_item(lines[d], v + 1)
        item = oriented(d, item)

        @pl.when(valid & (lines[d] == 0))
        def _():
            act(item, half, ())

        @pl.when(valid & (lines[d] > 0))
        def _():
            act(item, half, (d,))

    def sum_load(v):
        for d in range(2):

            def act(item, half, ups, d=d):
                @pl.when(half == 0)
                def _():
                    wait_part(item)

                for up in ups:
                    sum_copy(up, item, half, 0).wait_recv()
                for copy in loads(d, item, half, d, 0, ups):
                    copy.start()

            sum_cases(d, v, act)

    def sum_send(v):
        for d in range(2):

            def act(item, half, ups, d=d):
                for copy in loads(d, item, half, d, 0, ups):
                    copy.wait()
                add(d, lax.rem(v + 1, 2), ups)
                sum_copy(d, item, half, v + 1).start()

            sum_cases(d, v, act)

    def item_of(k):
        line = jnp.where(z < 2, z, CHIPS - 1 - z)
        item = jnp.int32(0)
        for i, (a, b) in enumerate(zip((2, 4, 6, 7, 5, 3), (4, 6, 0, 7, 1, 5))):
            item = jnp.where(k == i + 1, jnp.where(line == 0, a, b), item)
        item = jnp.where(z < 2, item, mirror(item))
        return jnp.where(k == 0, own, jnp.where(k == SLOTS - 1, other, item))

    def x_copy(item):
        return pltpu.make_async_copy(xg.at[item], xv, x_sem)

    def w_copies(i):
        return [
            pltpu.make_async_copy(w.at[:, columns(i, ft)], v.at[i], w_sem.at[n, i])
            for n, (w, v) in enumerate(((wg, wgv), (wu, wuv)))
        ]

    def column_tile(t):
        return jnp.where(t < HALF, (1 - c) * HALF + t, c * HALF + t - HALF)

    def wd_copy(t):
        slot = lax.rem(t, HALF)
        return pltpu.make_async_copy(wd.at[:, columns(column_tile(t), nt)], wdv.at[slot], wd_sem.at[slot])

    def stash_copy(item, t):
        return pltpu.make_async_copy(sst.at[t], stash.at[item, t], stash_sem.at[t])

    def wait_stored(item):
        for t in range(HALF):
            stash_copy(item, t).wait()
            part_copy(item, partner, t, part_send.at[t]).wait_send()

    barrier = pltpu.get_barrier_semaphore()

    def greet(device):
        pl.semaphore_signal(barrier, inc=1, device_id={"tp": device}, device_id_type=pl.DeviceIdType.MESH)

    greet(partner)
    for d in range(2):

        @pl.when(lines[d] <= CHIPS - 2)
        def _():
            greet(targets[d])

    pl.semaphore_wait(barrier, 1 + jnp.where(z > 0, 1, 0) + jnp.where(z < CHIPS - 1, 1, 0))

    def first_copy(n, half):
        at = rows_of(half, 1 - c if n == 0 else c)
        sem = (ag_recv if n == 0 else d2d_recv).at[own, half]
        return remote(x.at[at], xg.at[own, at], first_sem.at[n, half], sem, partner)

    def first_unit(unit):
        for d in range(2):

            @pl.when(lines[d] <= CHIPS - 2)
            def _():
                start_gather(d, 2 * z, unit, unit)

    for half in range(2):
        first_copy(0, half).start()

    @pl.when(c == 0)
    def _():
        first_unit(0)
        first_unit(1)

    for half in range(2):
        first_copy(1, half).start()
    pltpu.make_async_copy(x, xv, x_sem).start()

    @pl.loop(0, TILES)
    def _(i):
        for copy in w_copies(i):
            copy.start()

    for t in range(HALF):
        wd_copy(jnp.int32(t)).start()
    for half in range(2):
        wait_gathered(other, half)

        @pl.when(c == 1)
        def _():
            first_unit(half)

    pltpu.make_async_copy(x, xv, x_sem).wait()

    @pl.loop(0, SLOTS)
    def _(k):
        item, following = item_of(k), item_of(k + 1)

        @pl.when(k > 0)
        def _():
            x_copy(item).wait()
            wait_stored(item)

        @pl.loop(0, TILES)
        def _(i):
            @pl.when(k == 0)
            def _():
                for copy in w_copies(i):
                    copy.wait()

            @pl.when((i == 2))
            def _():
                gather_service(2 * k + 1)

            @pl.when((i == 0) | (i == 2))
            def _():
                sum_load(2 * k + lax.div(i, 2))

            @pl.when((i == 1) | (i == 3))
            def _():
                sum_send(2 * k + lax.div(i, 2))

            gate = jnp.dot(xv[...], wgv[i], preferred_element_type=jnp.float32)
            up = jnp.dot(xv[...], wuv[i], preferred_element_type=jnp.float32)
            hv[:, columns(i, ft)] = (jax.nn.gelu(gate) * up).astype(jnp.bfloat16)

        def down(t):
            wd_copy(t).wait()
            return jnp.dot(hv[...], wdv[lax.rem(t, HALF)], preferred_element_type=jnp.float32)

        @pl.loop(0, HALF)
        def _(t):
            @pl.when(t == 1)
            def _():
                gather_service(2 * k + 2)

            pst[t] = down(t).astype(jnp.bfloat16)
            part_copy(item, partner, t, part_send.at[t]).start()
            wd_copy(t + HALF).start()

        @pl.loop(0, HALF)
        def _(t):
            @pl.when((t == 1) & (k < SLOTS - 1))
            def _():
                for half in range(2):
                    pass_on(0, following, half, 0, 1 - c).wait_recv()
                x_copy(following).start()

            sst[t] = down(t + HALF)
            stash_copy(item, t).start()

            @pl.when(k < SLOTS - 1)
            def _():
                wd_copy(t).start()

    wait_stored(other)
    for d in range(2):

        @pl.when(sends(d, jnp.int32(LAST)))
        def _():
            gather_copy(d, own, 0, LAST, xg.at[own, rows_of(0, c)]).wait_send()

    for n in range(2):
        for half in range(2):
            first_copy(n, half).wait_send()

    def final_cases(act):
        @pl.when(z == 0)
        def _():
            act((1,))

        @pl.when((z > 0) & (z < CHIPS - 1))
        def _():
            act((0, 1))

        @pl.when(z == CHIPS - 1)
        def _():
            act((0,))

    def final_load(f):
        core, half = f // 2, f % 2
        if half == 0:
            wait_part(2 * z + core)

        def act(ups):
            for up in ups:
                sum_copy(up, 2 * z + core, half, 0).wait_recv()
            for copy in loads(f % 2, 2 * z + core, half, f % 2, 0, ups):
                copy.start()

        final_cases(act)

    def y_at(half, t):
        return y.at[chunk(half), columns(c * HALF + t, nt)]

    def final_store(f):
        core, half = f // 2, f % 2

        def act(ups):
            for copy in loads(f % 2, 2 * z + core, half, f % 2, 0, ups):
                copy.wait()
            add(f % 2, core, ups)

        final_cases(act)

        @pl.when(c == core)
        def _():
            for t in range(HALF):
                pltpu.make_async_copy(c_out.at[half, core, t], y_at(half, t), y_local.at[half, t]).start()

        @pl.when(c != core)
        def _():
            for t in range(HALF):
                y_copy(core, half, t).start()

    def y_copy(core, half, t):
        return remote(c_out.at[half, core, t], y_at(half, t), y_send.at[half, t], y_recv.at[half, t], partner)

    final_load(0)
    for f in range(4):
        if f < 3:
            final_load(f + 1)
        final_store(f)
    for half in range(2):
        for t in range(HALF):
            pltpu.make_async_copy(c_out.at[half, 0, t], y_at(half, t), y_local.at[half, t]).wait()
            y_copy(0, half, t).wait_send()
            y_copy(0, half, t).wait_recv()


def block(x, w_gate, w_up, w_down):
    rows, depth = x.shape
    width, out = w_gate.shape[1], w_down.shape[1]
    ft, nt = width // TILES, out // TILES
    bf16, f32 = jnp.bfloat16, jnp.float32
    half_rows = rows // 2
    shape = jax.ShapeDtypeStruct
    any_space = pl.BlockSpec(memory_space=pl.ANY)
    dma = pltpu.SemaphoreType.DMA
    results = pl.pallas_call(
        kernel,
        name="mlp_block",
        out_shape=[
            shape((rows, out), bf16),
            shape((SLOTS, rows, depth), bf16),
            shape((SLOTS, HALF, rows, nt), f32),
            shape((SLOTS, HALF, rows, nt), bf16),
            shape((SLOTS, HALF, rows, nt), bf16),
            shape((SLOTS, HALF, rows, nt), bf16),
        ],
        in_specs=[any_space] * 4,
        out_specs=[any_space] * 6,
        scratch_shapes=[
            pltpu.VMEM((rows, depth), bf16),
            pltpu.VMEM((rows, width), bf16),
            pltpu.VMEM((TILES, depth, ft), bf16),
            pltpu.VMEM((TILES, depth, ft), bf16),
            pltpu.VMEM((HALF, width, nt), bf16),
            pltpu.VMEM((HALF, rows, nt), bf16),
            pltpu.VMEM((HALF, rows, nt), f32),
            pltpu.VMEM((2, HALF, half_rows, nt), f32),
            pltpu.VMEM((2, HALF, half_rows, nt), bf16),
            pltpu.VMEM((2, 2, HALF, half_rows, nt), bf16),
            pltpu.VMEM((2, 2, HALF, half_rows, nt), bf16),
            dma(()),
            dma((2, TILES)),
            dma((HALF,)),
            dma((2, 2)),
            dma((SLOTS, 2)),
            dma((SLOTS, 2)),
            dma((2, 2)),
            dma((2, 2)),
            dma((HALF,)),
            dma((SLOTS,)),
            dma((HALF,)),
            dma((2, 4)),
            dma((2, SLOTS, 2)),
            dma((2, HALF)),
            dma((2, HALF)),
            dma((2, HALF)),
        ],
        compiler_params=pltpu.CompilerParams(
            collective_id=0, has_side_effects=True, vmem_limit_bytes=67_043_328
        ),
    )(x, w_gate, w_up, w_down)
    return results[0]


def solution(mesh):
    return jax.shard_map(
        block,
        mesh=mesh,
        in_specs=(P(("dp", "tp"), None), P(None, "tp"), P(None, "tp"), P("tp", None)),
        out_specs=P(("dp", "tp"), None),
        check_vma=False,
    )
```

time: 545 us -> 217 us (0.40)
  waiting for transfers between devices: 332 us -> 0 us
  Pallas kernels: 0 us -> 213 us
  matrix products: 199 us -> 0 us
  between operations: 13.4 us -> 0.01 us
    pallas_call x0 -> x1, Pallas kernels: none -> 213 us  [block(): pl.pallas_call(kernel, name='mlp_block', out_shape=[shape((rows, out), bf...]
    dot_general x3 -> x0, matrix products: 199 us -> none  [the longest x1 74 us: step(): up = jnp.dot(rows, w_up, preferred_element_type=jnp.float32)]
    reduce_scatter x1 -> x0, waiting for transfers between devices: 172 us -> none  [step(): return lax.psum_scatter(term, 'tp', scatter_dimension=0, tiled=True)]
    all_gather x1 -> x0, waiting for transfers between devices: 160 us -> none  [step(): rows = lax.all_gather(x, 'tp', axis=0, tiled=True)]
  transfers between devices with their start and end apart: 2 -> 0, of which waited for: 2 -> 0; matrix products, arithmetic and copies ran while one was open for 0% -> 0% of each run, Pallas kernels for 0% -> 0%
where the time goes in v1:
time: 217 us; the launch traced here: 216 us
  Pallas kernels  213 us (98%)
  local copies, waits for them, and re-layouts  3.09 us (1%)
    pallas_call x1, Pallas kernels, block(): pl.pallas_call(kernel, name='mlp_block', out_shape=[shape((rows, out), bf...  213 us

profile of v1, /device:TPU:0, one launch (start us, length us, event | category | flops | bytes accessed | tf_op | source)
XLA Modules:
  0.0 216.0 jit_solution(2457960052742445605)
XLA Ops:
  0.0 212.9 %mlp_block.1 = (bf16[352,3072]{1,0:T(8,128)(2,1)}, bf16[8,352,3072]{2,1,0:T(8,128)(2,1)}, f32[8,3,352,512]{3,2,1,0:T(8,128)}, bf16[8,3,352,512]{3,2,1,0:T(8,128)...) custom-call(bf16[352,3072]{1,0:T(8,128)(2,1)} %x.1, bf16[3072,3072]{1,0:T(8,128)(2,1)} %wg.1, ...), custom_call_target="tpu_custom_call" | custom-call | tf_op jit(solution)/shard_map/mlp_block/pallas_call | solution.py:421
  212.9 3.1 %copy.6 = bf16[352,3072]{1,0:T(8,128)(2,1)} copy(bf16[352,3072]{1,0:T(8,128)(2,1)} %get-tuple-element.6) | data formatting | bytes 4325376

commit v2 on v1

v2 whole, which is shorter than its diff:
```python
import functools

import jax
import jax.numpy as jnp
from jax import lax
from jax.experimental import pallas as pl
from jax.experimental.pallas import tpu as pltpu
from jax.sharding import PartitionSpec as P

CHIPS = 4
SLOTS = 2 * CHIPS
TILES = 6
HALF = TILES // 2


def mirror(item):
    return 6 - item + 2 * lax.rem(item, 2)


def gather_item(line, unit):
    slot = lax.div(unit, 2)
    item = jnp.where(slot <= line, 2 * (line - slot), 2 * (slot - line) - 1)
    return (line <= CHIPS - 2) & (slot < 2 * line + 2), item, lax.rem(unit, 2)


def sum_item(line, slot):
    at, ahead = slot - (2 * line + 2), CHIPS - 1 - line
    item = jnp.where(at < ahead, 2 * (line + 1 + at), 2 * (CHIPS - 1 - (at - ahead)) + 1)
    return (line <= CHIPS - 2) & (at >= 0) & (slot < SLOTS), item


def kernel(
    x, wg, wu, wd, y, xg, stash, part, from_left, from_right,
    xv, hv, wgv, wuv, wdv, pst, sst, c_own, c_part, c_up, c_out,
    x_sem, w_sem, wd_sem, first_sem, ag_recv, d2d_recv, d2d_send, send, part_send, part_recv,
    stash_sem, load_sem, sum_send_sem, sum_recv, fin_sem, y_local, y_send, y_recv,
):
    rows, depth = x.shape
    ft, nt = wg.shape[1] // TILES, wd.shape[1] // TILES
    assert ft == nt
    quarter, half_rows = rows // 4, rows // 2
    me = lax.axis_index("tp")
    z, c = lax.div(me, 2), lax.rem(me, 2)
    partner = me + 1 - 2 * c
    own, other = me, partner
    lines = (z, CHIPS - 1 - z)
    sources = (z - 1, CHIPS - 2 - z)
    targets = (me + 2, me - 2)
    sums = (from_left, from_right)

    def oriented(d, item):
        return item if d == 0 else mirror(item)

    def remote(src, dst, ssem, rsem, device):
        return pltpu.make_async_remote_copy(
            src_ref=src, dst_ref=dst, send_sem=ssem, recv_sem=rsem,
            device_id={"tp": device}, device_id_type=pl.DeviceIdType.MESH,
        )

    def rows_of(half, core):
        return pl.ds(pl.multiple_of((2 * half + core) * quarter, 8), quarter)

    def columns(i, size):
        return pl.ds(pl.multiple_of(i * size, size), size)

    def gather_copy(d, item, half, src):
        return remote(src, xg.at[item, rows_of(half, c)], send.at[d, half], ag_recv.at[item, half], targets[d])

    def start_gather(d, item, half):
        @pl.when(item == own)
        def _():
            gather_copy(d, item, half, x.at[rows_of(half, c)]).start()

        @pl.when(item != own)
        def _():
            gather_copy(d, item, half, xg.at[item, rows_of(half, c)]).start()

    def wait_gathered(item, half):
        gather_copy(0, item, half, xg.at[item, rows_of(half, c)]).wait_recv()

    def pass_on(d, item, half, core):
        at = xg.at[item, rows_of(half, core)]
        return remote(at, at, d2d_send.at[d, half], d2d_recv.at[item, half], partner)

    def gather_service(v):
        for d in range(2):
            valid, item, half = gather_item(sources[d], v - 2)
            item = oriented(d, item)

            @pl.when(valid & (v >= 2))
            def _():
                pass_on(d, item, half, c).wait_send()

            valid, item, half = gather_item(sources[d], v - 1)
            item = oriented(d, item)

            @pl.when(valid)
            def _():
                wait_gathered(item, half)
                pass_on(d, item, half, c).start()

        for d in range(2):
            valid, item, half = gather_item(lines[d], v - 1)

            @pl.when(valid)
            def _():
                gather_copy(d, own, half, xg.at[own, rows_of(half, c)]).wait_send()

            valid, item, half = gather_item(lines[d], v + 1)
            item = oriented(d, item)

            @pl.when(valid)
            def _():
                start_gather(d, item, half)

    def loads(d, item, t, ups):
        pairs = [(stash.at[item, t], c_own.at[d]), (part.at[item, t], c_part.at[d])]
        pairs += [(sums[up].at[item, t], c_up.at[d]) for up in ups]
        return [pltpu.make_async_copy(a, b, load_sem.at[d, i]) for i, (a, b) in enumerate(pairs)]

    def part_copy(item, t):
        return remote(pst.at[t], part.at[item, t], part_send.at[t], part_recv.at[item, t], partner)

    def sum_copy(d, item, t):
        return remote(
            c_out.at[d, t], sums[d].at[item, t], sum_send_sem.at[d, t], sum_recv.at[d, item, t], targets[d]
        )

    def add(own_ref, others, out):
        step = rows // 11 if rows % 176 == 0 else 16

        @pl.loop(0, rows // step)
        def _(i):
            at = pl.ds(pl.multiple_of(i * step, 16), step)
            total = own_ref[at, :]
            for ref in others:
                total += ref[at, :].astype(jnp.float32)
            out[at, :] = total.astype(jnp.bfloat16)

    def sum_cases(d, slot, act):
        valid, item = sum_item(lines[d], slot)
        item = oriented(d, item)

        @pl.when(valid & (lines[d] == 0))
        def _():
            act(item, ())

        @pl.when(valid & (lines[d] > 0))
        def _():
            act(item, (d,))

    def stored(t):
        stash_copy(own, t).wait()
        part_copy(own, t).wait_send()

    def sum_load(slot, t):
        for d in range(2):

            def act(item, ups, d=d):
                part_copy(item, t).wait_recv()
                for up in ups:
                    sum_copy(up, item, t).wait_recv()
                for copy in loads(d, item, t, ups):
                    copy.start()

            sum_cases(d, slot, act)

    def sum_send(slot, t):
        for d in range(2):

            @pl.when(sum_item(lines[d], slot - 1)[0])
            def _():
                sum_copy(d, own, t).wait_send()

            def act(item, ups, d=d):
                for copy in loads(d, item, t, ups):
                    copy.wait()
                add(c_own.at[d], [c_part.at[d]] + [c_up.at[d] for _ in ups], c_out.at[d, t])
                sum_copy(d, item, t).start()

            sum_cases(d, slot, act)

    def item_of(k):
        line = jnp.where(z < 2, z, CHIPS - 1 - z)
        item = jnp.int32(0)
        for i, (a, b) in enumerate(zip((2, 4, 6, 7, 5, 3), (4, 6, 0, 7, 1, 5))):
            item = jnp.where(k == i + 1, jnp.where(line == 0, a, b), item)
        item = jnp.where(z < 2, item, mirror(item))
        return jnp.where(k == 0, own, jnp.where(k == SLOTS - 1, other, item))

    def x_copy(item, half):
        at = pl.ds(half * half_rows, half_rows)
        return pltpu.make_async_copy(xg.at[item, at], xv.at[at], x_sem.at[half])

    def x_load(item, half):
        pass_on(0, item, half, 1 - c).wait_recv()
        x_copy(item, half).start()

    def w_copies(i):
        return [
            pltpu.make_async_copy(w.at[:, columns(i, ft)], v.at[i], w_sem.at[n, i])
            for n, (w, v) in enumerate(((wg, wgv), (wu, wuv)))
        ]

    def wd_copies(pair):
        t, base = lax.rem(pair, HALF), 2 * lax.rem(pair, 2)
        return [
            pltpu.make_async_copy(
                wd.at[:, columns(core * HALF + t, nt)], wdv.at[base + j], wd_sem.at[base + j]
            )
            for j, core in enumerate((c, 1 - c))
        ]

    def stash_copy(item, t):
        return pltpu.make_async_copy(sst.at[t], stash.at[item, t], stash_sem.at[t])

    x_first = pltpu.make_async_copy(x, xv, x_sem.at[0])
    x_first.start()
    for copy in w_copies(0):
        copy.start()
    barrier = pltpu.get_barrier_semaphore()

    def greet(device):
        pl.semaphore_signal(barrier, inc=1, device_id={"tp": device}, device_id_type=pl.DeviceIdType.MESH)

    greet(partner)
    for d in range(2):

        @pl.when(lines[d] <= CHIPS - 2)
        def _():
            greet(targets[d])

    pl.semaphore_wait(barrier, 1 + jnp.where(z > 0, 1, 0) + jnp.where(z < CHIPS - 1, 1, 0))

    def first_copy(n, half):
        at = rows_of(half, 1 - c if n == 0 else c)
        sem = (ag_recv if n == 0 else d2d_recv).at[own, half]
        return remote(x.at[at], xg.at[own, at], first_sem.at[n, half], sem, partner)

    def first_unit(unit):
        for d in range(2):

            @pl.when(lines[d] <= CHIPS - 2)
            def _():
                start_gather(d, 2 * z, unit)

    for half in range(2):
        first_copy(0, half).start()

    @pl.when(c == 0)
    def _():
        first_unit(0)
        first_unit(1)

    for half in range(2):
        first_copy(1, half).start()

    @pl.loop(1, TILES)
    def _(i):
        for copy in w_copies(i):
            copy.start()

    for pair in range(2):
        for copy in wd_copies(jnp.int32(pair)):
            copy.start()
    for half in range(2):
        wait_gathered(other, half)

        @pl.when(c == 1)
        def _():
            first_unit(half)

    x_first.wait()

    spare = pl.ds(0, rows)

    def final_cases(act):
        @pl.when(z == 0)
        def _():
            act((1,))

        @pl.when((z > 0) & (z < CHIPS - 1))
        def _():
            act((0, 1))

        @pl.when(z == CHIPS - 1)
        def _():
            act((0,))

    def part_in(item, t):
        n = lax.rem(item, 2) * HALF + t
        return pltpu.make_async_copy(part.at[item, t], wgv.at[n, spare], fin_sem.at[n, 0])

    def part_load(item, t):
        part_copy(item, t).wait_recv()
        part_in(item, t).start()

    def own_load(t):
        return pltpu.make_async_copy(stash.at[own, t], c_own.at[t], fin_sem.at[t, 3])

    def up_in(core, t, up):
        n = core * HALF + t
        return pltpu.make_async_copy(
            sums[up].at[2 * z + core, t], wuv.at[n, pl.ds(up * rows, rows)], fin_sem.at[n, 1 + up]
        )

    def up_load(core, t):
        def act(ups):
            for up in ups:
                sum_copy(up, 2 * z + core, t).wait_recv()
                up_in(core, t, up).start()

        final_cases(act)

    def final_early():
        for t in range(HALF):
            own_load(t).start()
            part_load(other, t)
            up_load(0, t)

    def staged(core, t):
        return hv.at[:, columns(core * HALF + t, nt)]

    def y_at(t):
        return y.at[:, columns(c * HALF + t, nt)]

    def y_stay(core, t):
        return pltpu.make_async_copy(staged(core, t), y_at(t), y_local.at[t])

    def y_leave(core, t):
        return remote(staged(core, t), y_at(t), y_send.at[t], y_recv.at[t], partner)

    def final_store(core, t):
        n = core * HALF + t

        def act(ups):
            part_in(2 * z + core, t).wait()
            for up in ups:
                up_in(core, t, up).wait()
            others = [wgv.at[n, spare]] + [wuv.at[n, pl.ds(up * rows, rows)] for up in ups]

            @pl.when(c == core)
            def _():
                own_load(t).wait()
                add(c_own.at[t], others, staged(core, t))
                y_stay(core, t).start()

            @pl.when(c != core)
            def _():
                add(sst.at[t], others, staged(core, t))
                y_leave(core, t).start()

        final_cases(act)

    @pl.loop(0, SLOTS)
    def _(k):
        item, following = item_of(k), item_of(k + 1)

        def gate_up(n, at):
            gate = jnp.dot(xv[at, :], wgv[n], preferred_element_type=jnp.float32)
            up = jnp.dot(xv[at, :], wuv[n], preferred_element_type=jnp.float32)
            hv[at, columns(n, ft)] = (jax.nn.gelu(gate) * up).astype(jnp.bfloat16)

        def prefetch(t):
            for copy in wd_copies(HALF * k + t):
                copy.start()

        @pl.when(k == 0)
        def _():
            @pl.loop(0, HALF)
            def _(i):
                for j in range(2):
                    for copy in w_copies(2 * i + j):
                        copy.wait()
                for j in range(2):
                    gate_up(2 * i + j, pl.ds(0, rows))

        @pl.when(k > 0)
        def _():
            sum_send(k, 0)
            stored(1)
            sum_load(k, 1)
            x_copy(item, 0).wait()

            @pl.loop(0, TILES)
            def _(i):
                half = lax.div(i, HALF)

                @pl.when(i == 1)
                def _():
                    gather_service(2 * k)

                @pl.when((i == 1) | (i == 3))
                def _():
                    sum_send(k, lax.div(i + 1, 2))

                @pl.when(i == 2)
                def _():
                    stored(2)
                    sum_load(k, 2)
                    x_load(item, 1)

                @pl.when(i == HALF)
                def _():
                    x_copy(item, 1).wait()

                @pl.when((i == HALF) | (i == HALF + 1))
                def _():
                    prefetch(i - HALF)

                for j in range(2):
                    at = pl.ds(pl.multiple_of(half * half_rows, 16), half_rows)
                    gate_up(2 * lax.rem(i, HALF) + j, at)

        @pl.loop(0, HALF)
        def _(t):
            @pl.when(t == 0)
            def _():
                gather_service(2 * k + 1)

            @pl.when((k < SLOTS - 1) & (t == jnp.where(k == 0, 1, 2)))
            def _():
                x_load(following, 0)

            @pl.when(t == 2)
            def _():
                stored(0)
                sum_load(k + 1, 0)

            @pl.when((k == SLOTS - 1) & (t == 0))
            def _():
                final_early()

            @pl.when((k == SLOTS - 1) & (t == 2))
            def _():
                part_load(own, 0)

            pair = HALF * k + t
            base = 2 * lax.rem(pair, 2)
            for copy in wd_copies(pair):
                copy.wait()
            mine = jnp.dot(hv[...], wdv[base], preferred_element_type=jnp.float32)
            theirs = jnp.dot(hv[...], wdv[base + 1], preferred_element_type=jnp.float32)
            sst[t] = mine
            pst[t] = theirs.astype(jnp.bfloat16)
            stash_copy(item, t).start()
            part_copy(item, t).start()

            @pl.when(t == 0)
            def _():
                prefetch(2)

    part_load(own, 1)
    up_load(1, 0)
    part_load(own, 2)
    up_load(1, 1)
    for t in range(HALF):
        final_store(0, t)
    final_store(1, 0)
    up_load(1, 2)
    final_store(1, 1)
    final_store(1, 2)
    for t in range(1, HALF):
        stored(t)
    for d in range(2):

        @pl.when(lines[d] <= CHIPS - 2)
        def _():
            for t in range(HALF):
                sum_copy(d, own, t).wait_send()

    for n in range(2):
        for half in range(2):
            first_copy(n, half).wait_send()
    for t in range(HALF):
        y_stay(0, t).wait()
        y_leave(0, t).wait_send()
        y_leave(0, t).wait_recv()


def block(x, w_gate, w_up, w_down):
    rows, depth = x.shape
    width, out = w_gate.shape[1], w_down.shape[1]
    ft, nt = width // TILES, out // TILES
    bf16, f32 = jnp.bfloat16, jnp.float32
    shape = jax.ShapeDtypeStruct
    any_space = pl.BlockSpec(memory_space=pl.ANY)
    dma = pltpu.SemaphoreType.DMA
    results = pl.pallas_call(
        kernel,
        name="mlp_block",
        out_shape=[
            shape((rows, out), bf16),
            shape((SLOTS, rows, depth), bf16),
            shape((SLOTS, HALF, rows, nt), f32),
            shape((SLOTS, HALF, rows, nt), bf16),
            shape((SLOTS, HALF, rows, nt), bf16),
            shape((SLOTS, HALF, rows, nt), bf16),
        ],
        in_specs=[any_space] * 4,
        out_specs=[any_space] * 6,
        scratch_shapes=[
            pltpu.VMEM((rows, depth), bf16),
            pltpu.VMEM((rows, width), bf16),
            pltpu.VMEM((TILES, depth, ft), bf16),
            pltpu.VMEM((TILES, depth, ft), bf16),
            pltpu.VMEM((4, width, nt), bf16),
            pltpu.VMEM((HALF, rows, nt), bf16),
            pltpu.VMEM((HALF, rows, nt), f32),
            pltpu.VMEM((HALF, rows, nt), f32),
            pltpu.VMEM((2, rows, nt), bf16),
            pltpu.VMEM((2, rows, nt), bf16),
            pltpu.VMEM((2, HALF, rows, nt), bf16),
            dma((2,)),
            dma((2, TILES)),
            dma((4,)),
            dma((2, 2)),
            dma((SLOTS, 2)),
            dma((SLOTS, 2)),
            dma((2, 2)),
            dma((2, 2)),
            dma((HALF,)),
            dma((SLOTS, HALF)),
            dma((HALF,)),
            dma((2, 3)),
            dma((2, HALF)),
            dma((2, SLOTS, HALF)),
            dma((TILES, 4)),
            dma((HALF,)),
            dma((HALF,)),
            dma((HALF,)),
        ],
        compiler_params=pltpu.CompilerParams(
            collective_id=0, has_side_effects=True, vmem_limit_bytes=67_043_328
        ),
    )(x, w_gate, w_up, w_down)
    return results[0]


def solution(mesh):
    return jax.shard_map(
        block,
        mesh=mesh,
        in_specs=(P(("dp", "tp"), None), P(None, "tp"), P(None, "tp"), P("tp", None)),
        out_specs=P(("dp", "tp"), None),
        check_vma=False,
    )
```

time: 217 us -> 202 us (0.931)
  Pallas kernels: 213 us -> 199 us
    pallas_call x1, Pallas kernels: 213 us -> 199 us  [block(): pl.pallas_call(kernel, name='mlp_block', out_shape=[shape((rows, out), bf...]
where the time goes in v2:
time: 202 us
  Pallas kernels  199 us (99%)
  local copies, waits for them, and re-layouts  3.09 us (2%)
    pallas_call x1, Pallas kernels, block(): pl.pallas_call(kernel, name='mlp_block', out_shape=[shape((rows, out), bf...  199 us

profile of v2, /device:TPU:0, one launch (start us, length us, event | category | flops | bytes accessed | tf_op | source)
XLA Modules:
  0.0 201.9 jit_solution(15162798160565235953)
XLA Ops:
  0.0 198.8 %mlp_block.1 = (bf16[352,3072]{1,0:T(8,128)(2,1)}, bf16[8,352,3072]{2,1,0:T(8,128)(2,1)}, f32[8,3,352,512]{3,2,1,0:T(8,128)}, bf16[8,3,352,512]{3,2,1,0:T(8,128)...) custom-call(bf16[352,3072]{1,0:T(8,128)(2,1)} %x.1, bf16[3072,3072]{1,0:T(8,128)(2,1)} %wg.1, ...), custom_call_target="tpu_custom_call" | custom-call | tf_op jit(solution)/shard_map/mlp_block/pallas_call | solution.py:489
  198.9 3.1 %copy.6 = bf16[352,3072]{1,0:T(8,128)(2,1)} copy(bf16[352,3072]{1,0:T(8,128)(2,1)} %get-tuple-element.6) | data formatting | bytes 4325376

commit v3 on v2

--- a/solution.py
+++ b/solution.py
@@ -33,7 +33,7 @@
     x, wg, wu, wd, y, xg, stash, part, from_left, from_right,
     xv, hv, wgv, wuv, wdv, pst, sst, c_own, c_part, c_up, c_out,
     x_sem, w_sem, wd_sem, first_sem, ag_recv, d2d_recv, d2d_send, send, part_send, part_recv,
-    stash_sem, load_sem, sum_send_sem, sum_recv, fin_sem, y_local, y_send, y_recv,
+    stash_sem, load_sem, sum_send_sem, sum_recv, y_sem,
 ):
     rows, depth = x.shape
     ft, nt = wg.shape[1] // TILES, wd.shape[1] // TILES
@@ -119,12 +119,27 @@
         return [pltpu.make_async_copy(a, b, load_sem.at[d, i]) for i, (a, b) in enumerate(pairs)]
 
     def part_copy(item, t):
-        return remote(pst.at[t], part.at[item, t], part_send.at[t], part_recv.at[item, t], partner)
+        return remote(pst.at[t], part.at[item, t], part_send.at[0, t], part_recv.at[item, t], partner)
+
+    def part_rest(t):
+        at = xv.at[:, columns(t, nt)]
+        return remote(at, part.at[me, t], part_send.at[1, t], part_recv.at[me, t], partner)
+
+    def sum_sem(d, chip, index, t):
+        both = lax.div(index, 2) == chip
+        return sum_recv.at[jnp.where(both & (d == 1), SLOTS + lax.rem(index, 2), index), t]
 
     def sum_copy(d, item, t):
+        ends = lax.div(item, 2) == lax.div(targets[d], 2)
+        index, device = jnp.where(ends, targets[d], item), jnp.where(ends, item, targets[d])
         return remote(
-            c_out.at[d, t], sums[d].at[item, t], sum_send_sem.at[d, t], sum_recv.at[d, item, t], targets[d]
+            c_out.at[d, t], sums[d].at[index, t], sum_send_sem.at[d, t],
+            sum_sem(d, lax.div(targets[d], 2), index, t), device,
         )
+
+    def wait_sum(d, index, t):
+        at = sums[d].at[index, t]
+        remote(at, at, sum_send_sem.at[d, t], sum_sem(d, z, index, t), partner).wait_recv()
 
     def add(own_ref, others, out):
         step = rows // 11 if rows % 176 == 0 else 16
@@ -149,9 +164,17 @@
         def _():
             act(item, (d,))
 
-    def stored(t):
+    def stored(slot, t):
         stash_copy(own, t).wait()
-        part_copy(own, t).wait_send()
+
+        @pl.when(slot == 0)
+        def _():
+            stash_rest(t).wait()
+
+        @pl.when(slot > 0)
+        def _():
+            part_copy(own, t).wait_send()
+
 
     def sum_load(slot, t):
         for d in range(2):
@@ -159,7 +182,7 @@
             def act(item, ups, d=d):
                 part_copy(item, t).wait_recv()
                 for up in ups:
-                    sum_copy(up, item, t).wait_recv()
+                    wait_sum(up, item, t)
                 for copy in loads(d, item, t, ups):
                     copy.start()
 
@@ -212,7 +235,10 @@
         ]
 
     def stash_copy(item, t):
-        return pltpu.make_async_copy(sst.at[t], stash.at[item, t], stash_sem.at[t])
+        return pltpu.make_async_copy(sst.at[t], stash.at[item, t], stash_sem.at[0, t])
+
+    def stash_rest(t):
+        return pltpu.make_async_copy(c_own.at[t], stash.at[other, t], stash_sem.at[1, t])
 
     x_first = pltpu.make_async_copy(x, xv, x_sem.at[0])
     x_first.start()
@@ -229,8 +255,9 @@
         @pl.when(lines[d] <= CHIPS - 2)
         def _():
             greet(targets[d])
-
-    pl.semaphore_wait(barrier, 1 + jnp.where(z > 0, 1, 0) + jnp.where(z < CHIPS - 1, 1, 0))
+            greet(targets[d] + 1 - 2 * c)
+
+    pl.semaphore_wait(barrier, 1 + jnp.where(z > 0, 2, 0) + jnp.where(z < CHIPS - 1, 2, 0))
 
     def first_copy(n, half):
         at = rows_of(half, 1 - c if n == 0 else c)
@@ -287,68 +314,56 @@
         def _():
             act((0,))
 
-    def part_in(item, t):
-        n = lax.rem(item, 2) * HALF + t
-        return pltpu.make_async_copy(part.at[item, t], wgv.at[n, spare], fin_sem.at[n, 0])
-
-    def part_load(item, t):
-        part_copy(item, t).wait_recv()
-        part_in(item, t).start()
-
-    def own_load(t):
-        return pltpu.make_async_copy(stash.at[own, t], c_own.at[t], fin_sem.at[t, 3])
-
-    def up_in(core, t, up):
-        n = core * HALF + t
+    def own_ref(h, t):
+        return c_own.at[t] if h == 0 else sst.at[t]
+
+    def final_copy(h, t, i):
+        n, index = h * HALF + t, 2 * z + h
+        if i == 0:
+            src, dst = stash.at[index, t], own_ref(h, t)
+        elif i == 1:
+            src, dst = part.at[index, t], wgv.at[n, spare]
+        else:
+            src, dst = sums[i - 2].at[index, t], wuv.at[n, pl.ds((i - 2) * rows, rows)]
+        sem = (
+            w_sem.at[0, n],
+            w_sem.at[1, n],
+            load_sem.at[h, t],
+            d2d_send.at[h, t] if t < HALF - 1 else x_sem.at[h],
+        )[i]
+        return pltpu.make_async_copy(src, dst, sem)
+
+    def part_load(t, rest):
+        for h in range(2):
+
+            @pl.when((h == c) == (rest == 0))
+            def _():
+                part_copy(2 * z + h, t).wait_recv()
+                final_copy(h, t, 1).start()
+
+    def up_load(t):
+        def act(ups):
+            for h in range(2):
+                for up in ups:
+                    wait_sum(up, 2 * z + h, t)
+                    final_copy(h, t, 2 + up).start()
+
+        final_cases(act)
+
+    def y_copy(h, t):
         return pltpu.make_async_copy(
-            sums[up].at[2 * z + core, t], wuv.at[n, pl.ds(up * rows, rows)], fin_sem.at[n, 1 + up]
+            hv.at[:, columns(h * HALF + t, nt)], y.at[:, columns(h * HALF + t, nt)], y_sem
         )
 
-    def up_load(core, t):
+    def final_store(t):
         def act(ups):
-            for up in ups:
-                sum_copy(up, 2 * z + core, t).wait_recv()
-                up_in(core, t, up).start()
-
-        final_cases(act)
-
-    def final_early():
-        for t in range(HALF):
-            own_load(t).start()
-            part_load(other, t)
-            up_load(0, t)
-
-    def staged(core, t):
-        return hv.at[:, columns(core * HALF + t, nt)]
-
-    def y_at(t):
-        return y.at[:, columns(c * HALF + t, nt)]
-
-    def y_stay(core, t):
-        return pltpu.make_async_copy(staged(core, t), y_at(t), y_local.at[t])
-
-    def y_leave(core, t):
-        return remote(staged(core, t), y_at(t), y_send.at[t], y_recv.at[t], partner)
-
-    def final_store(core, t):
-        n = core * HALF + t
-
-        def act(ups):
-            part_in(2 * z + core, t).wait()
-            for up in ups:
-                up_in(core, t, up).wait()
-            others = [wgv.at[n, spare]] + [wuv.at[n, pl.ds(up * rows, rows)] for up in ups]
-
-            @pl.when(c == core)
-            def _():
-                own_load(t).wait()
-                add(c_own.at[t], others, staged(core, t))
-                y_stay(core, t).start()
-
-            @pl.when(c != core)
-            def _():
-                add(sst.at[t], others, staged(core, t))
-                y_leave(core, t).start()
+            for h in range(2):
+                n = h * HALF + t
+                for i in (0, 1, *(2 + up for up in ups)):
+                    final_copy(h, t, i).wait()
+                others = [wgv.at[n, spare]] + [wuv.at[n, pl.ds(up * rows, rows)] for up in ups]
+                add(own_ref(h, t), others, hv.at[:, columns(n, nt)])
+                y_copy(h, t).start()
 
         final_cases(act)
 
@@ -378,90 +393,127 @@
         @pl.when(k > 0)
         def _():
             sum_send(k, 0)
-            stored(1)
+            stored(k - 1, 1)
             sum_load(k, 1)
             x_copy(item, 0).wait()
 
-            @pl.loop(0, TILES)
-            def _(i):
-                half = lax.div(i, HALF)
-
-                @pl.when(i == 1)
-                def _():
-                    gather_service(2 * k)
-
-                @pl.when((i == 1) | (i == 3))
-                def _():
-                    sum_send(k, lax.div(i + 1, 2))
-
-                @pl.when(i == 2)
-                def _():
-                    stored(2)
-                    sum_load(k, 2)
-                    x_load(item, 1)
-
-                @pl.when(i == HALF)
-                def _():
-                    x_copy(item, 1).wait()
-
-                @pl.when((i == HALF) | (i == HALF + 1))
-                def _():
-                    prefetch(i - HALF)
-
-                for j in range(2):
-                    at = pl.ds(pl.multiple_of(half * half_rows, 16), half_rows)
-                    gate_up(2 * lax.rem(i, HALF) + j, at)
-
-        @pl.loop(0, HALF)
-        def _(t):
-            @pl.when(t == 0)
-            def _():
-                gather_service(2 * k + 1)
-
-            @pl.when((k < SLOTS - 1) & (t == jnp.where(k == 0, 1, 2)))
-            def _():
-                x_load(following, 0)
-
-            @pl.when(t == 2)
-            def _():
-                stored(0)
-                sum_load(k + 1, 0)
-
-            @pl.when((k == SLOTS - 1) & (t == 0))
-            def _():
-                final_early()
-
-            @pl.when((k == SLOTS - 1) & (t == 2))
-            def _():
-                part_load(own, 0)
-
-            pair = HALF * k + t
+            upper, lower = (pl.ds(half * half_rows, half_rows) for half in range(2))
+            for n in range(2):
+                gate_up(n, upper)
+            gather_service(2 * k)
+            sum_send(k, 1)
+            for n in range(2, 4):
+                gate_up(n, upper)
+            x_load(item, 1)
+            for n in range(4, TILES):
+                gate_up(n, upper)
+            stored(k - 1, 2)
+            sum_load(k, 2)
+            x_copy(item, 1).wait()
+            prefetch(0)
+            for n in range(2):
+                gate_up(n, lower)
+            sum_send(k, 2)
+            prefetch(1)
+            for n in range(2, TILES):
+                gate_up(n, lower)
+
+        def down(pair):
             base = 2 * lax.rem(pair, 2)
             for copy in wd_copies(pair):
                 copy.wait()
-            mine = jnp.dot(hv[...], wdv[base], preferred_element_type=jnp.float32)
-            theirs = jnp.dot(hv[...], wdv[base + 1], preferred_element_type=jnp.float32)
-            sst[t] = mine
-            pst[t] = theirs.astype(jnp.bfloat16)
-            stash_copy(item, t).start()
-            part_copy(item, t).start()
-
-            @pl.when(t == 0)
-            def _():
-                prefetch(2)
-
-    part_load(own, 1)
-    up_load(1, 0)
-    part_load(own, 2)
-    up_load(1, 1)
+            return tuple(
+                jnp.dot(hv[...], wdv[base + j], preferred_element_type=jnp.float32) for j in range(2)
+            )
+
+        @pl.when(k == 0)
+        def _():
+            @pl.loop(0, HALF)
+            def _(t):
+                @pl.when(t == 0)
+                def _():
+                    gather_service(1)
+
+                @pl.when(t == 1)
+                def _():
+                    x_load(following, 0)
+
+                @pl.when(t == 2)
+                def _():
+                    stored(0, 0)
+
+                mine, theirs = down(t)
+                sst[t] = mine
+                c_own[t] = theirs
+                stash_copy(own, t).start()
+                stash_rest(t).start()
+
+                @pl.when(t == 0)
+                def _():
+                    prefetch(2)
+
+        @pl.when(k > 0)
+        def _():
+            kept = jnp.where(k < SLOTS - 1, item, SLOTS)
+
+            def tile_pair(t):
+                mine, theirs = down(HALF * k + t)
+                sst[t] = mine
+                pst[t] = theirs.astype(jnp.bfloat16)
+                stash_copy(kept, t).start()
+                part_copy(item, t).start()
+
+            def send_rest(t):
+                add(sst.at[t], [], xv.at[:, columns(t, nt)])
+                part_rest(t).start()
+
+            gather_service(2 * k + 1)
+
+            @pl.when(k == SLOTS - 1)
+            def _():
+                for n in range(HALF):
+                    final_copy(0, n, 0).start()
+                up_load(0)
+
+            tile_pair(0)
+            prefetch(2)
+            tile_pair(1)
+
+            @pl.when(k < SLOTS - 1)
+            def _():
+                x_load(following, 0)
+
+            stored(k, 0)
+            sum_load(k + 1, 0)
+
+            @pl.when(k == SLOTS - 1)
+            def _():
+                for t in range(2):
+                    send_rest(t)
+                final_copy(1, 0, 0).start()
+                part_load(0, 0)
+                up_load(1)
+
+            tile_pair(2)
+
+            @pl.when(k == SLOTS - 1)
+            def _():
+                send_rest(2)
+
+    stored(jnp.int32(SLOTS - 1), 1)
+    final_copy(1, 1, 0).start()
+    part_load(0, 1)
+    for t in range(1, HALF):
+        for rest in range(2):
+            part_load(t, rest)
+    stored(jnp.int32(SLOTS - 1), 2)
+    final_copy(1, 2, 0).start()
+    final_store(0)
+    final_store(1)
+    up_load(2)
+    final_store(2)
     for t in range(HALF):
-        final_store(0, t)
-    final_store(1, 0)
-    up_load(1, 2)
-    final_store(1, 1)
-    final_store(1, 2)
-    for t in range(1, HALF):
-        stored(t)
+        part_rest(t).wait_send()
     for d in range(2):
 
         @pl.when(lines[d] <= CHIPS - 2)
@@ -472,10 +524,7 @@
     for n in range(2):
         for half in range(2):
             first_copy(n, half).wait_send()
-    for t in range(HALF):
-        y_stay(0, t).wait()
-        y_leave(0, t).wait_send()
-        y_leave(0, t).wait_recv()
+    pltpu.make_async_copy(hv, y, y_sem).wait()
 
 
 def block(x, w_gate, w_up, w_down):
@@ -492,7 +541,7 @@
         out_shape=[
             shape((rows, out), bf16),
             shape((SLOTS, rows, depth), bf16),
-            shape((SLOTS, HALF, rows, nt), f32),
+            shape((SLOTS + 1, HALF, rows, nt), f32),
             shape((SLOTS, HALF, rows, nt), bf16),
             shape((SLOTS, HALF, rows, nt), bf16),
             shape((SLOTS, HALF, rows, nt), bf16),
@@ -519,16 +568,13 @@
             dma((SLOTS, 2)),
             dma((2, 2)),
             dma((2, 2)),
-            dma((HALF,)),
+            dma((2, HALF)),
             dma((SLOTS, HALF)),
-            dma((HALF,)),
+            dma((2, HALF)),
             dma((2, 3)),
             dma((2, HALF)),
-            dma((2, SLOTS, HALF)),
-            dma((TILES, 4)),
-            dma((HALF,)),
-            dma((HALF,)),
-            dma((HALF,)),
+            dma((SLOTS + 2, HALF)),
+            dma(()),
         ],
         compiler_params=pltpu.CompilerParams(
             collective_id=0, has_side_effects=True, vmem_limit_bytes=67_043_328

time: 202 us -> 200 us (0.990)
  Pallas kernels: 199 us -> 196 us
    pallas_call x1, Pallas kernels: 199 us -> 196 us  [block(): pl.pallas_call(kernel, name='mlp_block', out_shape=[shape((rows, out), bf...]
where the time goes in v3:
time: 200 us; the launch traced here: 199 us
  Pallas kernels  196 us (98%)
  local copies, waits for them, and re-layouts  3.09 us (2%)
    pallas_call x1, Pallas kernels, block(): pl.pallas_call(kernel, name='mlp_block', out_shape=[shape((rows, out), bf...  196 us

profile of v3, /device:TPU:0, one launch (start us, length us, event | category | flops | bytes accessed | tf_op | source)
XLA Modules:
  0.0 198.9 jit_solution(5305041555175586880)
XLA Ops:
  0.0 195.8 %mlp_block.1 = (bf16[352,3072]{1,0:T(8,128)(2,1)}, bf16[8,352,3072]{2,1,0:T(8,128)(2,1)}, f32[9,3,352,512]{3,2,1,0:T(8,128)}, bf16[8,3,352,512]{3,2,1,0:T(8,128)...) custom-call(bf16[352,3072]{1,0:T(8,128)(2,1)} %x.1, bf16[3072,3072]{1,0:T(8,128)(2,1)} %wg.1, ...), custom_call_target="tpu_custom_call" | custom-call | tf_op jit(solution)/shard_map/mlp_block/pallas_call | solution.py:538
  195.8 3.1 %copy.6 = bf16[352,3072]{1,0:T(8,128)(2,1)} copy(bf16[352,3072]{1,0:T(8,128)(2,1)} %get-tuple-element.6) | data formatting | bytes 4325376

commit v4 on v3

--- a/solution.py
+++ b/solution.py
@@ -33,7 +33,7 @@
     x, wg, wu, wd, y, xg, stash, part, from_left, from_right,
     xv, hv, wgv, wuv, wdv, pst, sst, c_own, c_part, c_up, c_out,
     x_sem, w_sem, wd_sem, first_sem, ag_recv, d2d_recv, d2d_send, send, part_send, part_recv,
-    stash_sem, load_sem, sum_send_sem, sum_recv, y_sem,
+    stash_sem, load_sem, sum_send_sem, sum_recv, y_sem, free_sem, up_free,
 ):
     rows, depth = x.shape
     ft, nt = wg.shape[1] // TILES, wd.shape[1] // TILES
@@ -121,9 +121,15 @@
     def part_copy(item, t):
         return remote(pst.at[t], part.at[item, t], part_send.at[0, t], part_recv.at[item, t], partner)
 
+    def landing(h, t):
+        return wgv.at[h * HALF + t, pl.ds(0, rows)]
+
+    def part_last(t):
+        return remote(pst.at[t], landing(1 - c, t), part_send.at[0, t], part_recv.at[other, t], partner)
+
     def part_rest(t):
         at = xv.at[:, columns(t, nt)]
-        return remote(at, part.at[me, t], part_send.at[1, t], part_recv.at[me, t], partner)
+        return remote(at, landing(c, t), part_send.at[1, t], part_recv.at[me, t], partner)
 
     def sum_sem(d, chip, index, t):
         both = lax.div(index, 2) == chip
@@ -152,6 +158,16 @@
                 total += ref[at, :].astype(jnp.float32)
             out[at, :] = total.astype(jnp.bfloat16)
 
+    def sum_last(d):
+        chip = lax.div(targets[d], 2)
+        return remote(
+            c_out.at[d, HALF - 1], up_landing(c, d), sum_send_sem.at[d, HALF - 1],
+            sum_sem(d, chip, targets[d], HALF - 1), 2 * chip + 1,
+        )
+
+    def up_landing(h, d):
+        return wuv.at[h, pl.ds((2 + d) * rows, rows)]
+
     def sum_cases(d, slot, act):
         valid, item = sum_item(lines[d], slot)
         item = oriented(d, item)
@@ -165,14 +181,14 @@
             act(item, (d,))
 
     def stored(slot, t):
-        stash_copy(own, t).wait()
-
         @pl.when(slot == 0)
         def _():
+            stash_copy(own, t).wait()
             stash_rest(t).wait()
 
-        @pl.when(slot > 0)
-        def _():
+        @pl.when((slot > 0) & (slot < SLOTS - 1))
+        def _():
+            stash_copy(own, t).wait()
             part_copy(own, t).wait_send()
 
 
@@ -188,7 +204,7 @@
 
             sum_cases(d, slot, act)
 
-    def sum_send(slot, t):
+    def sum_send(slot, t, last=False):
         for d in range(2):
 
             @pl.when(sum_item(lines[d], slot - 1)[0])
@@ -199,7 +215,11 @@
                 for copy in loads(d, item, t, ups):
                     copy.wait()
                 add(c_own.at[d], [c_part.at[d]] + [c_up.at[d] for _ in ups], c_out.at[d, t])
-                sum_copy(d, item, t).start()
+                if last:
+                    pl.semaphore_wait(up_free.at[d], 1)
+                    sum_last(d).start()
+                else:
+                    sum_copy(d, item, t).start()
 
             sum_cases(d, slot, act)
 
@@ -321,32 +341,27 @@
         n, index = h * HALF + t, 2 * z + h
         if i == 0:
             src, dst = stash.at[index, t], own_ref(h, t)
-        elif i == 1:
-            src, dst = part.at[index, t], wgv.at[n, spare]
         else:
-            src, dst = sums[i - 2].at[index, t], wuv.at[n, pl.ds((i - 2) * rows, rows)]
+            src, dst = sums[i - 1].at[index, t], wuv.at[n, pl.ds((i - 1) * rows, rows)]
         sem = (
             w_sem.at[0, n],
-            w_sem.at[1, n],
             load_sem.at[h, t],
             d2d_send.at[h, t] if t < HALF - 1 else x_sem.at[h],
         )[i]
         return pltpu.make_async_copy(src, dst, sem)
-
-    def part_load(t, rest):
-        for h in range(2):
-
-            @pl.when((h == c) == (rest == 0))
-            def _():
-                part_copy(2 * z + h, t).wait_recv()
-                final_copy(h, t, 1).start()
 
     def up_load(t):
         def act(ups):
             for h in range(2):
                 for up in ups:
                     wait_sum(up, 2 * z + h, t)
-                    final_copy(h, t, 2 + up).start()
+                    if t < HALF - 1:
+                        final_copy(h, t, 1 + up).start()
+                    else:
+
+                        @pl.when(c == 0)
+                        def _():
+                            final_copy(h, t, 1 + up).start()
 
         final_cases(act)
 
@@ -359,10 +374,22 @@
         def act(ups):
             for h in range(2):
                 n = h * HALF + t
-                for i in (0, 1, *(2 + up for up in ups)):
-                    final_copy(h, t, i).wait()
-                others = [wgv.at[n, spare]] + [wuv.at[n, pl.ds(up * rows, rows)] for up in ups]
-                add(own_ref(h, t), others, hv.at[:, columns(n, nt)])
+                part_copy(2 * z + h, t).wait_recv()
+                final_copy(h, t, 0).wait()
+
+                def total(refs, n=n, h=h):
+                    add(own_ref(h, t), [wgv.at[n, spare]] + refs, hv.at[:, columns(n, nt)])
+
+                def loaded(h=h, n=n, total=total):
+                    for up in ups:
+                        final_copy(h, t, 1 + up).wait()
+                    total([wuv.at[n, pl.ds(up * rows, rows)] for up in ups])
+
+                if t < HALF - 1:
+                    loaded()
+                else:
+                    pl.when(c == 0)(loaded)
+                    pl.when(c == 1)(lambda h=h, total=total: total([up_landing(h, up) for up in ups]))
                 y_copy(h, t).start()
 
         final_cases(act)
@@ -413,7 +440,24 @@
             prefetch(0)
             for n in range(2):
                 gate_up(n, lower)
-            sum_send(k, 2)
+
+            @pl.when(k < SLOTS - 1)
+            def _():
+                sum_send(k, 2)
+
+            @pl.when((k == SLOTS - 1) & (c == 1))
+            def _():
+                for d in range(2):
+
+                    @pl.when(sources[d] >= 0)
+                    def _():
+                        for core in range(2):
+                            pl.semaphore_signal(
+                                up_free.at[d], inc=1,
+                                device_id={"tp": 2 * (z - 1 if d == 0 else z + 1) + core},
+                                device_id_type=pl.DeviceIdType.MESH,
+                            )
+
             prefetch(1)
             for n in range(2, TILES):
                 gate_up(n, lower)
@@ -454,16 +498,18 @@
 
         @pl.when(k > 0)
         def _():
-            kept = jnp.where(k < SLOTS - 1, item, SLOTS)
-
             def tile_pair(t):
                 mine, theirs = down(HALF * k + t)
                 sst[t] = mine
                 pst[t] = theirs.astype(jnp.bfloat16)
-                stash_copy(kept, t).start()
-                part_copy(item, t).start()
+
+                @pl.when(k < SLOTS - 1)
+                def _():
+                    stash_copy(item, t).start()
+                    part_copy(item, t).start()
 
             def send_rest(t):
+                part_last(t).start()
                 add(sst.at[t], [], xv.at[:, columns(t, nt)])
                 part_rest(t).start()
 
@@ -471,9 +517,13 @@
 
             @pl.when(k == SLOTS - 1)
             def _():
+                sum_send(k, 2, last=True)
                 for n in range(HALF):
                     final_copy(0, n, 0).start()
                 up_load(0)
+                pl.semaphore_signal(
+                    free_sem, inc=1, device_id={"tp": partner}, device_id_type=pl.DeviceIdType.MESH
+                )
 
             tile_pair(0)
             prefetch(2)
@@ -488,10 +538,10 @@
 
             @pl.when(k == SLOTS - 1)
             def _():
+                pl.semaphore_wait(free_sem, 1)
                 for t in range(2):
                     send_rest(t)
-                final_copy(1, 0, 0).start()
-                part_load(0, 0)
+                    final_copy(1, t, 0).start()
                 up_load(1)
 
             tile_pair(2)
@@ -499,20 +549,14 @@
             @pl.when(k == SLOTS - 1)
             def _():
                 send_rest(2)
-
-    stored(jnp.int32(SLOTS - 1), 1)
-    final_copy(1, 1, 0).start()
-    part_load(0, 1)
-    for t in range(1, HALF):
-        for rest in range(2):
-            part_load(t, rest)
-    stored(jnp.int32(SLOTS - 1), 2)
-    final_copy(1, 2, 0).start()
+                final_copy(1, 2, 0).start()
+
     final_store(0)
     final_store(1)
     up_load(2)
     final_store(2)
     for t in range(HALF):
+        part_last(t).wait_send()
         part_rest(t).wait_send()
     for d in range(2):
 
@@ -541,7 +585,7 @@
         out_shape=[
             shape((rows, out), bf16),
             shape((SLOTS, rows, depth), bf16),
-            shape((SLOTS + 1, HALF, rows, nt), f32),
+            shape((SLOTS, HALF, rows, nt), f32),
             shape((SLOTS, HALF, rows, nt), bf16),
             shape((SLOTS, HALF, rows, nt), bf16),
             shape((SLOTS, HALF, rows, nt), bf16),
@@ -575,6 +619,8 @@
             dma((2, HALF)),
             dma((SLOTS + 2, HALF)),
             dma(()),
+            pltpu.SemaphoreType.REGULAR,
+            pltpu.SemaphoreType.REGULAR((2,)),
         ],
         compiler_params=pltpu.CompilerParams(
             collective_id=0, has_side_effects=True, vmem_limit_bytes=67_043_328

time: 200 us -> 198 us (0.990)
  Pallas kernels: 196 us -> 194 us
    pallas_call x1, Pallas kernels: 196 us -> 194 us  [block(): pl.pallas_call(kernel, name='mlp_block', out_shape=[shape((rows, out), bf...]
where the time goes in v4:
time: 198 us; the launch traced here: 197 us
  Pallas kernels  194 us (98%)
  local copies, waits for them, and re-layouts  3.09 us (2%)
    pallas_call x1, Pallas kernels, block(): pl.pallas_call(kernel, name='mlp_block', out_shape=[shape((rows, out), bf...  194 us

profile of v4, /device:TPU:0, one launch (start us, length us, event | category | flops | bytes accessed | tf_op | source)
XLA Modules:
  0.0 196.6 jit_solution(16633321262658455872)
XLA Ops:
  0.0 193.5 %mlp_block.1 = (bf16[352,3072]{1,0:T(8,128)(2,1)}, bf16[8,352,3072]{2,1,0:T(8,128)(2,1)}, f32[8,3,352,512]{3,2,1,0:T(8,128)}, bf16[8,3,352,512]{3,2,1,0:T(8,128)...) custom-call(bf16[352,3072]{1,0:T(8,128)(2,1)} %x.1, bf16[3072,3072]{1,0:T(8,128)(2,1)} %wg.1, ...), custom_call_target="tpu_custom_call" | custom-call | tf_op jit(solution)/shard_map/mlp_block/pallas_call | solution.py:582
  193.5 3.1 %copy.6 = bf16[352,3072]{1,0:T(8,128)(2,1)} copy(bf16[352,3072]{1,0:T(8,128)(2,1)} %get-tuple-element.6) | data formatting | bytes 4325376
